TPU v7x, 16 devices: a whole 2x2x2 slice. The times are simulated.
16 devices in a mesh: sub: 2 (over z), data: 8 (over y, x, core).
Axes of the slice: x: 2, y: 2, z: 2, core: 2. Of those that a mesh axis runs over, the one named last changes fastest.
Arguments:
- x_act: bfloat16 [96, 196, 512], P(('data', 'sub'))
- y_tgt: bfloat16 [96, 196, 512], P(('data', 'sub'))
- w_in: float32 [8, 512, 2048], replicated
- w_out: float32 [8, 2048, 512], replicated
Outputs:
- output 1: float32 [8, 512, 2048], replicated
- output 2: float32 [8, 2048, 512], replicated
- output 3: float32 [], replicated
All inputs are finite; a program needn't handle non-finite values.
Results may differ from a plain program's by a relative error of at most 0.00157091.
Values are sent between devices in bfloat16 or wider.
A program may use at most 1 GiB of HBM per device.

v0:
```python
import jax
import jax.numpy as jnp
from jax import lax
from jax.sharding import PartitionSpec as P

RHO_SCALE = 0.1
STEP_SIZE = 1.0


def gelu_exact(pre_act):
    return jax.nn.gelu(pre_act, approximate=False)


def local_pass(tok_in, tok_tgt, w_in_b, w_out_b):
    layers = w_in_b.shape[0]
    hidden = tok_in
    saved_acts = []
    for layer_idx in range(layers):
        pre_act = jnp.dot(hidden, w_in_b[layer_idx], preferred_element_type=jnp.float32).astype(jnp.bfloat16)
        gelu_out = gelu_exact(pre_act.astype(jnp.float32)).astype(jnp.bfloat16)
        branch = jnp.dot(gelu_out, w_out_b[layer_idx], preferred_element_type=jnp.float32)
        saved_acts.append((hidden, pre_act, gelu_out))
        hidden = (hidden.astype(jnp.float32) + branch).astype(jnp.bfloat16)
    res_diff = hidden.astype(jnp.float32) - tok_tgt.astype(jnp.float32)
    elem_count = res_diff.size
    loss_val = 0.5 * jnp.sum(res_diff * res_diff) / elem_count
    back_err = (res_diff / elem_count).astype(jnp.bfloat16)
    grads_in = []
    grads_out = []
    for layer_idx in reversed(range(layers)):
        hid_in, pre_act, gelu_out = saved_acts[layer_idx]
        grads_out.append(jnp.einsum("tf,td->fd", gelu_out, back_err, preferred_element_type=jnp.float32).astype(jnp.bfloat16))
        d_act = jnp.einsum("td,fd->tf", back_err, w_out_b[layer_idx], preferred_element_type=jnp.float32).astype(jnp.bfloat16)
        gelu_vjp = jax.vjp(gelu_exact, pre_act.astype(jnp.float32))[1]
        d_pre = gelu_vjp(d_act.astype(jnp.float32))[0].astype(jnp.bfloat16)
        grads_in.append(jnp.einsum("td,tf->df", hid_in, d_pre, preferred_element_type=jnp.float32).astype(jnp.bfloat16))
        if layer_idx > 0:
            back_err = (back_err.astype(jnp.float32) + jnp.einsum("tf,df->td", d_pre, w_in_b[layer_idx], preferred_element_type=jnp.float32)).astype(jnp.bfloat16)
    return loss_val, grads_in[::-1], grads_out[::-1]


def solution(mesh):
    sub_size = mesh.shape["sub"]
    dev_count = sub_size * mesh.shape["data"]

    def device_step(x_blk, y_blk, w_in, w_out):
        model_dim = w_in.shape[1]
        tok_in = x_blk.reshape(-1, model_dim)
        tok_tgt = y_blk.reshape(-1, model_dim)
        first_res = local_pass(tok_in, tok_tgt, w_in.astype(jnp.bfloat16), w_out.astype(jnp.bfloat16))
        wide_in = jnp.stack(first_res[1]).astype(jnp.float32)
        wide_out = jnp.stack(first_res[2]).astype(jnp.float32)
        sum_in, sum_out = lax.psum((wide_in, wide_out), "sub")
        mean_in = sum_in / sub_size
        mean_out = sum_out / sub_size
        grad_norm = jnp.sqrt(jnp.sum(mean_in * mean_in) + jnp.sum(mean_out * mean_out))
        eps_scale = RHO_SCALE * model_dim ** 0.5 / grad_norm
        pert_in = (w_in + eps_scale * mean_in).astype(jnp.bfloat16)
        pert_out = (w_out + eps_scale * mean_out).astype(jnp.bfloat16)
        second_res = local_pass(tok_in, tok_tgt, pert_in, pert_out)
        wide2_in = jnp.stack(second_res[1]).astype(jnp.float32)
        wide2_out = jnp.stack(second_res[2]).astype(jnp.float32)
        tot_in, tot_out, tot_loss = lax.psum((wide2_in, wide2_out, second_res[0]), ("sub", "data"))
        return (w_in - STEP_SIZE * (tot_in / dev_count), w_out - STEP_SIZE * (tot_out / dev_count), tot_loss / dev_count)

    batch_spec = P(("data", "sub"))
    return jax.shard_map(device_step, mesh=mesh, in_specs=(batch_spec, batch_spec, P(), P()), out_specs=(P(), P(), P()), check_vma=False)
```

profile of v0, /device:TPU:0, one launch (start us, length us, event | category | flops | bytes accessed | tf_op | source)
XLA Modules:
  0.0 3329.9 jit_solution(4040208427437569558)
XLA Ops:
  5.3 17.6 convert_element_type.634
  38.7 22.4 fusion.58
  69.3 22.7 fusion.87
  99.1 23.2 fusion.116
  130.2 22.8 fusion.145
  161.0 22.8 fusion.174
  191.6 22.8 fusion.203
  222.3 23.2 fusion.232
  255.0 22.8 fusion.261
  299.2 11.4 fusion.274
  402.5 13.4 fusion.647
  500.5 10.5 fusion.675
  515.3 31.7 copy.22
  547.0 1504.5 %all-reduce.4 = (f32[8,512,2048]{1,2,0:T(8,128)}, f32[8,2048,512]{2,1,0:T(8,128)}) all-reduce(bf16[8,512,2048]{1,2,0:T(8,128)(2,1)} %fusion.661, bf16[8,2048,512]{2,1,0:T(8,128)(2,1)} %fusion.677), channel_id=1, replica_groups=mesh['sub'=2,'data'=8] {'sub'}, use_global_device_ids=true, to_apply=%region_0.0 | all-reduce | flops 16777216 | bytes 100663296 | tf_op jit(solution)/shard_map/psum | solution.py:53
  2051.5 16.4 multiply_reduce_fusion
  2082.3 27.4 add_convert_fusion
  2109.8 27.5 add_convert_fusion.1
  2137.3 22.7 fusion.350
  2168.1 23.2 fusion.379
  2198.3 23.3 fusion.408
  2229.8 23.3 fusion.437
  2260.8 23.5 fusion.466
  2292.0 23.6 fusion.495
  2323.2 23.7 fusion.524
  2356.5 23.2 fusion.553
  2404.2 11.4 fusion.566
  2506.9 13.6 fusion.679
  2604.1 10.6 fusion.707
  2619.0 610.8 %all-reduce.5 = (f32[8,512,2048]{1,2,0:T(8,128)}, f32[8,2048,512]{2,1,0:T(8,128)}, f32[]{:T(128)}) all-reduce(bf16[8,512,2048]{1,2,0:T(8,128)(2,1)} %fusion.693, bf16[8,2048,512]{2,1,0:T(8,128)(2,1)} %fusion.709, f32[]{:T(128)S(6)} %div.47), channel_id=1, replica_groups=mesh['sub'=2,'data'=8] {'sub','data'}, use_global_device_ids=true, to_apply=%region_4.0 | all-reduce | flops 16777216 | bytes 100663304 | tf_op jit(solution)/shard_map/psum | solution.py:63
  3230.4 33.2 multiply_subtract_fusion.1
  3263.6 31.7 copy.23
  3295.2 33.2 multiply_subtract_fusion
  (430 shorter events, 549.1 us)
Async XLA Ops:
  2.1 59.2 %copy-start.16 = (bf16[1176,512]{1,0:T(8,128)(2,1)}, bf16[1176,512]{1,0:T(8,128)(2,1)S(1)}, u32[]{:S(2)}) copy-start(bf16[1176,512]{1,0:T(8,128)(2,1)S(1)} %reshape.12) | copy-start | bytes 3612676
  5.2 26.2 copy-start
  69.3 22.7 copy-start.55
  255.0 22.8 copy-start.12
  255.0 22.8 copy-start.2
  293.6 24.9 slice-start.6
  293.6 24.9 slice-start.66
  299.1 19.4 slice-start.7
  299.1 19.4 slice-start.8
  299.1 19.4 slice-start.9
  299.1 19.4 slice-start.67
  299.2 19.4 slice-start.68
  327.7 24.6 slice-start.57
  361.6 24.7 slice-start.48
  491.9 19.2 slice-start
  491.9 19.1 slice-start.1
  491.9 19.1 slice-start.14
  2051.5 20.2 copy-start.1
  2109.7 27.5 copy-start.18
  2168.1 23.2 copy-start.48
  2356.4 23.3 copy-start.14
  2356.5 23.3 copy-start.3
  2398.7 24.5 slice-start.10
  2398.7 24.5 slice-start.39
  2404.1 19.0 slice-start.11
  2404.1 19.0 slice-start.12
  2404.2 19.0 slice-start.13
  2404.2 19.0 slice-start.40
  2404.2 19.0 slice-start.41
  2432.3 24.6 slice-start.30
  2466.3 24.6 slice-start.21
  2596.4 18.3 slice-start.3
  (129 other events, 1191.8 us)
where the time goes:
time: 3340 us; the launch traced here: 3330 us
  blocking collectives  2120 us (63%)
  matrix products  939 us (28%)
  other arithmetic  172 us (5%)
  local copies, waits for them, and re-layouts  96.9 us (3%)
    psum x1, blocking collectives, device_step(): sum_in, sum_out = lax.psum((wide_in, wide_out), 'sub')  1500 us
    psum x1, blocking collectives, device_step(): lax.psum((wide2_in, wide2_out, second_res[0]), ('sub', 'data'))  611 us
    dot_general x16, matrix products, local_pass(): jnp.dot(hidden, w_in_b[layer_idx], preferred_element_type=jnp.float32)  369 us
    dot_general x14, matrix products, local_pass(): jnp.einsum('td,fd->tf', back_err, w_out_b[layer_idx], preferred_element_t...  136 us
    dot_general x16, matrix products, local_pass(): jnp.einsum('tf,td->fd', gelu_out, back_err, preferred_element_type=jnp.fl...  123 us
    dot_general x16, matrix products, local_pass(): jnp.dot(gelu_out, w_out_b[layer_idx], preferred_element_type=jnp.float32)  113 us
    dot_general x16, matrix products, local_pass(): jnp.einsum('td,tf->df', hid_in, d_pre, preferred_element_type=jnp.float32)  100 us
    dot_general x14, matrix products, local_pass(): jnp.einsum('tf,df->td', d_pre, w_in_b[layer_idx], preferred_element_type=...  97.6 us

commit v1 on v0

v1 whole, which is shorter than its diff:
```python
import jax
import jax.numpy as jnp
from jax import lax
from jax.experimental.layout import Layout, with_layout_constraint
from jax.sharding import PartitionSpec as P

RHO_SCALE = 0.1
STEP_SIZE = 1.0
AXES = ("sub", "data")
F32, BF16 = jnp.float32, jnp.bfloat16


def gelu(z):
    return 0.5 * z * (1.0 + lax.erf(z * (0.5 ** 0.5)))


def gelu_slope(z):
    return 0.5 * (1.0 + lax.erf(z * (0.5 ** 0.5))) + z * (jnp.exp(-0.5 * z * z) * 0.3989422804014327)


def forward(hidden, w_in_b, w_out_b):
    saved = []
    for l in range(len(w_in_b)):
        pre = jnp.dot(hidden, w_in_b[l], preferred_element_type=F32).astype(BF16)
        act = gelu(pre.astype(F32)).astype(BF16)
        branch = jnp.dot(act, w_out_b[l], preferred_element_type=F32)
        saved.append((hidden, pre, act))
        hidden = (hidden.astype(F32) + branch).astype(BF16)
    return hidden, saved


def loss_and_err(hidden, target):
    diff = hidden.astype(F32) - target.astype(F32)
    return 0.5 * jnp.sum(diff * diff) / diff.size, (diff / diff.size).astype(BF16)


def rows_major(g):
    return with_layout_constraint(g, Layout(major_to_minor=(0, 1)))


def backward_layer(err, weights, saved, last):
    hid, pre, act = saved
    g_out = lax.dot_general(act, err, (((0,), (0,)), ((), ())), preferred_element_type=F32).astype(BF16)
    d_act = lax.dot_general(err, weights[1], (((1,), (1,)), ((), ())), preferred_element_type=F32).astype(BF16)
    d_pre = (gelu_slope(pre.astype(F32)) * d_act.astype(F32)).astype(BF16)
    g_in = lax.dot_general(hid, d_pre, (((0,), (0,)), ((), ())), preferred_element_type=F32).astype(BF16)
    if not last:
        err = (err.astype(F32) + lax.dot_general(d_pre, weights[0], (((1,), (1,)), ((), ())), preferred_element_type=F32)).astype(BF16)
    return err, rows_major(g_in), rows_major(g_out)


def solution(mesh):
    sub_size = mesh.shape["sub"]
    data_size = mesh.shape["data"]
    n = sub_size * data_size

    def flip(bit):
        return [(i, i ^ bit) for i in range(n)]

    regroup = []
    for i in range(n):
        z, yx, c = i // data_size, (i % data_size) // 2, i % 2
        regroup.append((i, c * data_size + yx * 2 + z))

    def device_step(x_blk, y_blk, w_in, w_out):
        layers, dim, _ = w_in.shape
        me = lax.axis_index("sub") * data_size + lax.axis_index("data")
        tok_in = lax.ppermute(x_blk.reshape(-1, dim), AXES, regroup)
        tok_tgt = lax.ppermute(y_blk.reshape(-1, dim), AXES, regroup)

        w_in_b, w_out_b = w_in.astype(BF16), w_out.astype(BF16)

        hidden, saved = forward(tok_in, w_in_b, w_out_b)
        err = loss_and_err(hidden, tok_tgt)[1]
        pair = [None] * layers
        waiting = None
        for l in reversed(range(layers)):
            away = waiting and [lax.ppermute(g, AXES, flip(1)) for g in waiting]
            grads = backward_layer(err, (w_in_b[l], w_out_b[l]), saved[l], l == 0)
            (err, g_in, g_out), away = lax.optimization_barrier((grads, away))
            if l + 1 < layers:
                pair[l + 1] = list(zip(waiting, away))
            waiting = (g_in, g_out)
        pair[0] = [(g, lax.ppermute(g, AXES, flip(1))) for g in waiting]
        mean = [[(a.astype(F32) + b.astype(F32)) / sub_size for a, b in p] for p in pair]
        squares = [jnp.sum((m * m).reshape(-1, 8, m.shape[1]), axis=0) for p in mean for m in p]
        norm_sq = sum(jnp.sum(q) for q in lax.optimization_barrier(squares))
        scale = RHO_SCALE * dim ** 0.5 / jnp.sqrt(norm_sq)
        pert_in = [(w_in[l] + scale * mean[l][0]).astype(BF16) for l in range(layers)]
        pert_out = [(w_out[l] + scale * mean[l][1]).astype(BF16) for l in range(layers)]

        axis_of = {8: 0, 4: 1, 2: 2, 1: 3}
        orders = ((1, 2, 4, 8), (1, 8, 4, 2))

        def halve(part, bit):
            mine = (me // bit) % 2
            ax = axis_of[bit]
            away = lax.ppermute(lax.dynamic_slice_in_dim(part, 1 - mine, 1, ax), AXES, flip(bit))
            return part, away

        def add(part, away, bit):
            return lax.dynamic_slice_in_dim(part, (me // bit) % 2, 1, axis_of[bit]).astype(F32) + away.astype(F32)

        def blocks(g):
            return g.reshape((2, 2, 2, 2, g.shape[0] // n, g.shape[1]))

        hidden, saved = forward(tok_in, pert_in, pert_out)
        loss, err = loss_and_err(hidden, tok_tgt)
        sums = [[None] * 2 for _ in range(layers)]
        pieces = [{}, {}]
        pipe = {}
        loss_bits = [1, 2, 4, 8]

        def gather(low, high):
            news = []
            for k, w in enumerate((w_in, w_out)):
                rows = w.shape[1] // n
                own = lax.dynamic_slice(w, (low, me * rows, 0), (high - low, rows, w.shape[2]))
                news.append(own - STEP_SIZE * (jnp.stack([s[k] for s in sums[low:high]]) / n))
            if low == 0:
                news, pieces[:] = lax.optimization_barrier((news, list(pieces)))
            for k, new in enumerate(news):
                pieces[k][low] = lax.all_gather(new, AXES, axis=1, tiled=True)

        for l in reversed(range(-4, layers)):
            sent = {(m, k, stage): halve(part, orders[k][stage]) for (m, k, stage), part in pipe.items()}
            more = lax.ppermute(loss, AXES, flip(loss_bits.pop(0))) if loss_bits else None
            grads = backward_layer(err, (pert_in[l], pert_out[l]), saved[l], l == 0) if l >= 0 else None
            grads, sent, more = lax.optimization_barrier((grads, sent, more))
            if more is not None:
                loss += more
            if l >= 0:
                err, g_in, g_out = grads
            pipe = {}
            for (m, k, stage), (part, away) in sent.items():
                part = add(part, away, orders[k][stage])
                if stage == 3:
                    sums[m][k] = part.reshape(part.shape[-2:])
                else:
                    pipe[m, k, stage + 1] = part
            if l >= 0:
                pipe[l, 0, 0], pipe[l, 1, 0] = blocks(g_in), blocks(g_out)
            for low, high in ((5, 8), (0, 5)):
                if l == low - 4:
                    gather(low, high)

        outs = [jnp.concatenate([p[low] for low in sorted(p)]) for p in pieces]
        return outs[0], outs[1], loss / n

    batch_spec = P(("data", "sub"))
    return jax.shard_map(device_step, mesh=mesh, in_specs=(batch_spec, batch_spec, P(), P()), out_specs=(P(), P(), P()), check_vma=False)
```

time: 3340 us -> 1360 us (0.41)
  blocking collectives: 2120 us -> 0 us
  waiting for transfers between devices: 0 us -> 338 us
  matrix products: 939 us -> 612 us
  starting transfers between devices: 0 us -> 79.9 us
  other arithmetic: 172 us -> 213 us
    psum x2 -> x0, blocking collectives: 2120 us -> none  [the longest x1 1500 us: device_step(): sum_in, sum_out = lax.psum((wide_in, wide_out), 'sub')]
    dot_general x92, matrix products: 939 us -> 612 us  [the longest x16 141 us: backward_layer(): lax.dot_general(act, err, (((0,), (0,)), ((), ())), preferred_element_typ...]
    ppermute x0 -> x86, waiting for transfers between devices: none -> 179 us  [the longest x64 179 us: halve(): lax.ppermute(lax.dynamic_slice_in_dim(part, 1 - mine, 1, ax), AXES, flip(...]
    all_gather x0 -> x4, waiting for transfers between devices: none -> 158 us  [gather(): pieces[k][low] = lax.all_gather(new, AXES, axis=1, tiled=True)]
    ppermute x0 -> x86, starting transfers between devices: none -> 79.7 us  [the longest x64 53.3 us: halve(): lax.ppermute(lax.dynamic_slice_in_dim(part, 1 - mine, 1, ax), AXES, flip(...]
    sub x2 -> x4, other arithmetic: 66.3 us -> 9.55 us  [gather(): own - STEP_SIZE * (jnp.stack([s[k] for s in sums[low:high]]) / n)]
    concatenate x0 -> x2, other arithmetic: none -> 47.1 us  [device_step(): outs = [jnp.concatenate([p[low] for low in sorted(p)]) for p in pieces]]
    unnamed x324 -> x516, local copies, waits for them, and re-layouts: 92.3 us -> 53.7 us
  transfers between devices with their start and end apart: 0 -> 90, of which waited for: 0 -> 32; matrix products, arithmetic and copies ran while one was open for 0% -> 32% of each run, Pallas kernels for 0% -> 0%
where the time goes in v1:
time: 1360 us; the launch traced here: 1350 us
  matrix products  612 us (45%)
  waiting for transfers between devices  338 us (25%)
  other arithmetic  213 us (16%)
  starting transfers between devices  79.9 us (6%)
  local copies, waits for them, and re-layouts  72 us (5%)
  between operations  32.4 us (2%)
    ppermute x64, waiting for transfers between devices, halve(): lax.ppermute(lax.dynamic_slice_in_dim(part, 1 - mine, 1, ax), AXES, flip(...  179 us
    all_gather x4, waiting for transfers between devices, gather(): pieces[k][low] = lax.all_gather(new, AXES, axis=1, tiled=True)  158 us
    dot_general x16, matrix products, backward_layer(): lax.dot_general(act, err, (((0,), (0,)), ((), ())), preferred_element_typ...  141 us
    dot_general x14, matrix products, backward_layer(): lax.dot_general(err, weights[1], (((1,), (1,)), ((), ())), preferred_elem...  127 us
    dot_general x16, matrix products, backward_layer(): lax.dot_general(hid, d_pre, (((0,), (0,)), ((), ())), preferred_element_t...  106 us
    dot_general x16, matrix products, forward(): branch = jnp.dot(act, w_out_b[l], preferred_element_type=F32)  96.6 us
    dot_general x16, matrix products, forward(): pre = jnp.dot(hidden, w_in_b[l], preferred_element_type=F32).astype(BF16)  81.6 us
    dot_general x14, matrix products, backward_layer(): lax.dot_general(d_pre, weights[0], (((1,), (1,)), ((), ())), preferred_el...  59.7 us
  transfers between devices with their start and end apart: 90, of which 32 were waited for; matrix products, arithmetic and copies ran while one was open for 32% of the time, Pallas kernels for 0%

profile of v1, /device:TPU:0, one launch (start us, length us, event | category | flops | bytes accessed | tf_op | source)
XLA Modules:
  0.0 1347.5 jit_solution(529043278349294249)
XLA Ops:
  9.6 10.8 collective-permute-start
  22.7 17.8 %convert_element_type.851 = bf16[8,512,2048]{2,1,0:T(8,128)(2,1)} convert(f32[8,512,2048]{2,1,0:T(8,128)} %param.6) | non-fusion elementwise | flops 8388608 | bytes 50331648 | tf_op jit(solution)/shard_map/convert_element_type | solution.py:71
  88.0 10.5 fusion.162
  116.6 10.4 fusion.164
  180.5 10.1 fusion.77
  203.0 9.6 fusion.68
  238.6 9.6 fusion.59
  262.9 10.3 convolution_convert_fusion.58
  276.0 9.4 fusion.50
  313.0 9.6 fusion.41
  336.7 10.3 convolution_convert_fusion.54
  374.0 9.4 convolution_convert_fusion.52
  384.8 9.4 fusion.23
  425.5 11.3 fusion.180
  475.6 22.2 %fusion.146 = (bf16[512,2048]{1,0:T(8,128)(2,1)}, bf16[512,2048]{1,0:T(8,128)(2,1)}, bf16[512,2048]{1,0:T(8,128)(2,1)}, bf16[512,2048]{1,0:T(8,128)(2,1)}, bf16[...) fusion(f32[8,512,2048]{2,1,0:T(8,128)} %param.6, bf16[512,2048]{1,0:T(8,128)(2,1)} %copy-done.12, ...), kind=kLoop, calls=%fused_computation.260 | loop fusion | flops 37748736 | bytes 62914564 | tf_op jit(solution)/shard_map/convert_element_type | solution.py:89
  503.9 20.8 %fusion.145 = (bf16[2048,512]{1,0:T(8,128)(2,1)}, bf16[2048,512]{1,0:T(8,128)(2,1)}, bf16[2048,512]{1,0:T(8,128)(2,1)}, bf16[2048,512]{1,0:T(8,128)(2,1)}, bf16[...) fusion(f32[8,2048,512]{2,1,0:T(8,128)} %param.7, bf16[2048,512]{1,0:T(8,128)(2,1)S(1)} %copy-done.8, ...), kind=kLoop, calls=%fused_computation.258 | loop fusion | flops 37748736 | bytes 62914564 | tf_op jit(solution)/shard_map/convert_element_type | solution.py:90
  530.6 10.6 fusion.157
  701.4 10.0 convolution_convert_fusion.42
  711.4 10.5 convolution_convert_fusion.40
  820.9 10.0 fusion.95
  864.2 9.9 convolution_convert_fusion.34
  939.4 12.4 fusion.181
  991.5 11.0 collective-permute-done.71
  1003.9 10.4 collective-permute-done.70
  1035.9 34.2 %collective-permute-done.78 = f32[1,1,1,1,32,2048]{5,4,3,2,1,0:T(8,128)S(1)} collective-permute-done((f32[1,1,1,1,32,2048]{5,4,3,2,1,0:T(8,128)S(1)}, f32[1,1,1,1,32,2048]{5,4,3,2,1,0:T(8,128)S(1)}, u32[]{:S(2)}, u32[]{:S(2)}) %collective-permute-start.78) | collective-permute-done | bytes 262176 | tf_op jit(solution)/shard_map/ppermute | solution.py:98
  1074.7 9.8 collective-permute-done.83
  1087.9 9.8 collective-permute-done.81
  1097.7 17.5 %collective-permute-done.80 = f32[2,1,1,1,32,2048]{5,4,3,2,1,0:T(8,128)S(1)} collective-permute-done((f32[2,1,1,1,32,2048]{5,4,3,2,1,0:T(8,128)S(1)}, f32[2,1,1,1,32,2048]{5,4,3,2,1,0:T(8,128)S(1)}, u32[]{:S(2)}, u32[]{:S(2)}) %collective-permute-start.80) | collective-permute-done | bytes 524320 | tf_op jit(solution)/shard_map/ppermute | solution.py:98
  1134.2 88.5 %all-gather.11.cloned.1.call-done = f32[5,2048,512]{2,1,0:T(8,128)} async-done(((f32[5,128,512]{2,1,0:T(8,128)}), f32[5,2048,512]{2,1,0:T(8,128)}) %all-gather.11.cloned.1.call-update) | async-done | bytes 20971536 | tf_op jit(solution)/shard_map/all_gather | solution.py:123
  1222.6 23.6 %pad_maximum_fusion.1 = f32[8,2048,512]{2,1,0:T(8,128)} fusion(f32[3,2048,512]{2,1,0:T(8,128)} %all-gather.7.cloned.1.call-done, f32[5,2048,512]{2,1,0:T(8,128)} %all-gather.11.cloned.1.call-done), kind=kLoop, calls=%fused_computation.1 | loop fusion | flops 8388608 | bytes 67108864 | tf_op jit(solution)/shard_map/concatenate | solution.py:147
  1246.3 69.6 %all-gather.9.cloned.1.call-done = f32[5,512,2048]{2,1,0:T(8,128)} async-done(((f32[5,32,2048]{2,1,0:T(8,128)}), f32[5,512,2048]{2,1,0:T(8,128)}) %all-gather.9.cloned.1.call-update) | async-done | bytes 20971536 | tf_op jit(solution)/shard_map/all_gather | solution.py:123
  1315.9 23.5 %pad_maximum_fusion = f32[8,512,2048]{2,1,0:T(8,128)} fusion(f32[3,512,2048]{2,1,0:T(8,128)} %all-gather.5.cloned.1.call-done, f32[5,512,2048]{2,1,0:T(8,128)} %all-gather.9.cloned.1.call-done), kind=kLoop, calls=%fused_computation | loop fusion | flops 8388608 | bytes 67108864 | tf_op jit(solution)/shard_map/concatenate | solution.py:147
  (945 shorter events, 762.2 us)
Async XLA Ops:
  7.2 1125.8 %all-gather.7.cloned.1.call-start = ((), (), s32[]{:S(2)}) async-start(), calls=%async_computation.1 | async-start | bytes 13369344 | tf_op jit(solution)/shard_map/all_gather | solution.py:123
  9.6 46.4 %collective-permute-start = (bf16[1176,512]{1,0:T(8,128)(2,1)}, bf16[1176,512]{1,0:T(8,128)(2,1)}, u32[]{:S(2)}, u32[]{:S(2)}) collective-permute-start(bf16[1176,512]{1,0:T(8,128)(2,1)} %reshape.108), channel_id=1, source_target_pairs={{0,0},{1,8},{2,2},{3,10},{4,4},{5,12},{6,6},{7,14},{8,1},{9,9},{10... | collective-permute-start | bytes 3612680 | tf_op jit(solution)/shard_map/ppermute | solution.py:68
  21.8 140.2 %collective-permute-start.1 = (bf16[1176,512]{1,0:T(8,128)(2,1)S(1)}, bf16[1176,512]{1,0:T(8,128)(2,1)S(1)}, u32[]{:S(2)}, u32[]{:S(2)}) collective-permute-start(bf16[1176,512]{1,0:T(8,128)(2,1)S(1)} %reshape.109), channel_id=1, source_target_pairs={{0,0},{1,8},{2,2},{3,10},{4,4},{5,12},{6,6},{7,14},{8,1},{9,9},{10... | collective-permute-start | bytes 3612680 | tf_op jit(solution)/shard_map/ppermute | solution.py:69
  676.6 34.8 %collective-permute-start.25 = (f32[1,2,2,1,128,512]{5,4,3,2,1,0:T(8,128)}, f32[1,2,2,1,128,512]{5,4,3,2,1,0:T(8,128)}, u32[]{:S(2)}, u32[]{:S(2)}) collective-permute-start(f32[1,2,2,1,128,512]{5,4,3,2,1,0:T(8,128)} %constant_dynamic-slice_fusion.58), channel_id=1, source_target_pairs={{0,8},{1,9},{2,10},{3,11},{4,12},{5,13},{6,14},{7,15},{8,0},{9,1},... | collective-permute-start | bytes 3145736 | tf_op jit(solution)/shard_map/ppermute | solution.py:98
  679.1 32.3 %collective-permute-start.24 = (f32[2,2,1,1,32,2048]{5,4,3,2,1,0:T(8,128)}, f32[2,2,1,1,32,2048]{5,4,3,2,1,0:T(8,128)}, u32[]{:S(2)}, u32[]{:S(2)}) collective-permute-start(f32[2,2,1,1,32,2048]{5,4,3,2,1,0:T(8,128)} %constant_dynamic-slice_fusion.59), channel_id=1, source_target_pairs={{0,2},{1,3},{2,0},{3,1},{4,6},{5,7},{6,4},{7,5},{8,10},{9,11},{10,... | collective-permute-start | bytes 3145736 | tf_op jit(solution)/shard_map/ppermute | solution.py:98
  736.2 23.4 %collective-permute-start.30 = (f32[1,2,2,1,128,512]{5,4,3,2,1,0:T(8,128)S(1)}, f32[1,2,2,1,128,512]{5,4,3,2,1,0:T(8,128)S(1)}, u32[]{:S(2)}, u32[]{:S(2)}) collective-permute-start(f32[1,2,2,1,128,512]{5,4,3,2,1,0:T(8,128)S(1)} %constant_dynamic-slice_fusion.54), channel_id=1, source_target_pairs={{0,8},{1,9},{2,10},{3,11},{4,12},{5,13},{6,14},{7,15},{8,0},{9,1},... | collective-permute-start | bytes 3145736 | tf_op jit(solution)/shard_map/ppermute | solution.py:98
  738.2 23.0 %collective-permute-start.29 = (f32[2,2,1,1,32,2048]{5,4,3,2,1,0:T(8,128)S(1)}, f32[2,2,1,1,32,2048]{5,4,3,2,1,0:T(8,128)S(1)}, u32[]{:S(2)}, u32[]{:S(2)}) collective-permute-start(f32[2,2,1,1,32,2048]{5,4,3,2,1,0:T(8,128)S(1)} %constant_dynamic-slice_fusion.55), channel_id=1, source_target_pairs={{0,2},{1,3},{2,0},{3,1},{4,6},{5,7},{6,4},{7,5},{8,10},{9,11},{10,... | collective-permute-start | bytes 3145736 | tf_op jit(solution)/shard_map/ppermute | solution.py:98
  786.0 24.0 %collective-permute-start.37 = (f32[1,2,2,1,128,512]{5,4,3,2,1,0:T(8,128)S(1)}, f32[1,2,2,1,128,512]{5,4,3,2,1,0:T(8,128)S(1)}, u32[]{:S(2)}, u32[]{:S(2)}) collective-permute-start(f32[1,2,2,1,128,512]{5,4,3,2,1,0:T(8,128)S(1)} %constant_dynamic-slice_fusion.48), channel_id=1, source_target_pairs={{0,8},{1,9},{2,10},{3,11},{4,12},{5,13},{6,14},{7,15},{8,0},{9,1},... | collective-permute-start | bytes 3145736 | tf_op jit(solution)/shard_map/ppermute | solution.py:98
  838.6 24.2 %collective-permute-start.45 = (f32[1,2,2,1,128,512]{5,4,3,2,1,0:T(8,128)S(1)}, f32[1,2,2,1,128,512]{5,4,3,2,1,0:T(8,128)S(1)}, u32[]{:S(2)}, u32[]{:S(2)}) collective-permute-start(f32[1,2,2,1,128,512]{5,4,3,2,1,0:T(8,128)S(1)} %constant_dynamic-slice_fusion.40), channel_id=1, source_target_pairs={{0,8},{1,9},{2,10},{3,11},{4,12},{5,13},{6,14},{7,15},{8,0},{9,1},... | collective-permute-start | bytes 3145736 | tf_op jit(solution)/shard_map/ppermute | solution.py:98
  840.1 22.7 %collective-permute-start.44 = (f32[2,2,1,1,32,2048]{5,4,3,2,1,0:T(8,128)S(1)}, f32[2,2,1,1,32,2048]{5,4,3,2,1,0:T(8,128)S(1)}, u32[]{:S(2)}, u32[]{:S(2)}) collective-permute-start(f32[2,2,1,1,32,2048]{5,4,3,2,1,0:T(8,128)S(1)} %constant_dynamic-slice_fusion.41), channel_id=1, source_target_pairs={{0,2},{1,3},{2,0},{3,1},{4,6},{5,7},{6,4},{7,5},{8,10},{9,11},{10,... | collective-permute-start | bytes 3145736 | tf_op jit(solution)/shard_map/ppermute | solution.py:98
  887.6 23.5 %collective-permute-start.53 = (f32[1,2,2,1,128,512]{5,4,3,2,1,0:T(8,128)S(1)}, f32[1,2,2,1,128,512]{5,4,3,2,1,0:T(8,128)S(1)}, u32[]{:S(2)}, u32[]{:S(2)}) collective-permute-start(f32[1,2,2,1,128,512]{5,4,3,2,1,0:T(8,128)S(1)} %constant_dynamic-slice_fusion.32), channel_id=1, source_target_pairs={{0,8},{1,9},{2,10},{3,11},{4,12},{5,13},{6,14},{7,15},{8,0},{9,1},... | collective-permute-start | bytes 3145736 | tf_op jit(solution)/shard_map/ppermute | solution.py:98
  889.3 23.1 %collective-permute-start.52 = (f32[2,2,1,1,32,2048]{5,4,3,2,1,0:T(8,128)S(1)}, f32[2,2,1,1,32,2048]{5,4,3,2,1,0:T(8,128)S(1)}, u32[]{:S(2)}, u32[]{:S(2)}) collective-permute-start(f32[2,2,1,1,32,2048]{5,4,3,2,1,0:T(8,128)S(1)} %constant_dynamic-slice_fusion.33), channel_id=1, source_target_pairs={{0,2},{1,3},{2,0},{3,1},{4,6},{5,7},{6,4},{7,5},{8,10},{9,11},{10,... | collective-permute-start | bytes 3145736 | tf_op jit(solution)/shard_map/ppermute | solution.py:98
  916.3 216.7 %all-gather.5.cloned.1.call-start = ((), (), s32[]{:S(2)}) async-start(), calls=%async_computation | async-start | bytes 13369344 | tf_op jit(solution)/shard_map/all_gather | solution.py:123
  921.6 301.1 %all-gather.11.cloned.1.call-start = ((), (), s32[]{:S(2)}) async-start(), calls=%async_computation.3 | async-start | bytes 22282240 | tf_op jit(solution)/shard_map/all_gather | solution.py:123
  923.8 29.5 %collective-permute-start.65 = (f32[1,1,1,1,128,512]{5,4,3,2,1,0:T(8,128)S(1)}, f32[1,1,1,1,128,512]{5,4,3,2,1,0:T(8,128)}, u32[]{:S(2)}, u32[]{:S(2)}) collective-permute-start(f32[1,1,1,1,128,512]{5,4,3,2,1,0:T(8,128)S(1)} %constant_dynamic-slice_fusion.20), channel_id=1, source_target_pairs={{0,2},{1,3},{2,0},{3,1},{4,6},{5,7},{6,4},{7,5},{8,10},{9,11},{10,... | collective-permute-start | bytes 786440 | tf_op jit(solution)/shard_map/ppermute | solution.py:98
  926.6 26.7 %collective-permute-start.64 = (f32[1,1,1,1,32,2048]{5,4,3,2,1,0:T(8,128)}, f32[1,1,1,1,32,2048]{5,4,3,2,1,0:T(8,128)}, u32[]{:S(2)}, u32[]{:S(2)}) collective-permute-start(f32[1,1,1,1,32,2048]{5,4,3,2,1,0:T(8,128)} %constant_dynamic-slice_fusion.21), channel_id=1, source_target_pairs={{0,8},{1,9},{2,10},{3,11},{4,12},{5,13},{6,14},{7,15},{8,0},{9,1},... | collective-permute-start | bytes 786440 | tf_op jit(solution)/shard_map/ppermute | solution.py:98
  929.9 24.0 %collective-permute-start.63 = (f32[1,1,2,1,128,512]{5,4,3,2,1,0:T(8,128)}, f32[1,1,2,1,128,512]{5,4,3,2,1,0:T(8,128)}, u32[]{:S(2)}, u32[]{:S(2)}) collective-permute-start(f32[1,1,2,1,128,512]{5,4,3,2,1,0:T(8,128)} %constant_dynamic-slice_fusion.22), channel_id=1, source_target_pairs={{0,4},{1,5},{2,6},{3,7},{4,0},{5,1},{6,2},{7,3},{8,12},{9,13},{10,... | collective-permute-start | bytes 1572872 | tf_op jit(solution)/shard_map/ppermute | solution.py:98
  933.5 39.0 %collective-permute-start.61 = (f32[1,2,2,1,128,512]{5,4,3,2,1,0:T(8,128)}, f32[1,2,2,1,128,512]{5,4,3,2,1,0:T(8,128)}, u32[]{:S(2)}, u32[]{:S(2)}) collective-permute-start(f32[1,2,2,1,128,512]{5,4,3,2,1,0:T(8,128)} %constant_dynamic-slice_fusion.24), channel_id=1, source_target_pairs={{0,8},{1,9},{2,10},{3,11},{4,12},{5,13},{6,14},{7,15},{8,0},{9,1},... | collective-permute-start | bytes 3145736 | tf_op jit(solution)/shard_map/ppermute | solution.py:98
  937.4 35.1 %collective-permute-start.60 = (f32[2,2,1,1,32,2048]{5,4,3,2,1,0:T(8,128)}, f32[2,2,1,1,32,2048]{5,4,3,2,1,0:T(8,128)}, u32[]{:S(2)}, u32[]{:S(2)}) collective-permute-start(f32[2,2,1,1,32,2048]{5,4,3,2,1,0:T(8,128)} %constant_dynamic-slice_fusion.25), channel_id=1, source_target_pairs={{0,2},{1,3},{2,0},{3,1},{4,6},{5,7},{6,4},{7,5},{8,10},{9,11},{10,... | collective-permute-start | bytes 3145736 | tf_op jit(solution)/shard_map/ppermute | solution.py:98
  977.3 25.1 %collective-permute-start.71 = (f32[1,1,2,1,128,512]{5,4,3,2,1,0:T(8,128)S(1)}, f32[1,1,2,1,128,512]{5,4,3,2,1,0:T(8,128)S(1)}, u32[]{:S(2)}, u32[]{:S(2)}) collective-permute-start(f32[1,1,2,1,128,512]{5,4,3,2,1,0:T(8,128)S(1)} %constant_dynamic-slice_fusion.14), channel_id=1, source_target_pairs={{0,4},{1,5},{2,6},{3,7},{4,0},{5,1},{6,2},{7,3},{8,12},{9,13},{10,... | collective-permute-start | bytes 1572872 | tf_op jit(solution)/shard_map/ppermute | solution.py:98
  979.2 41.9 %collective-permute-start.69 = (f32[1,2,2,1,128,512]{5,4,3,2,1,0:T(8,128)S(1)}, f32[1,2,2,1,128,512]{5,4,3,2,1,0:T(8,128)S(1)}, u32[]{:S(2)}, u32[]{:S(2)}) collective-permute-start(f32[1,2,2,1,128,512]{5,4,3,2,1,0:T(8,128)S(1)} %constant_dynamic-slice_fusion.16), channel_id=1, source_target_pairs={{0,8},{1,9},{2,10},{3,11},{4,12},{5,13},{6,14},{7,15},{8,0},{9,1},... | collective-permute-start | bytes 3145736 | tf_op jit(solution)/shard_map/ppermute | solution.py:98
  981.2 39.9 %collective-permute-start.68 = (f32[2,2,1,1,32,2048]{5,4,3,2,1,0:T(8,128)S(1)}, f32[2,2,1,1,32,2048]{5,4,3,2,1,0:T(8,128)S(1)}, u32[]{:S(2)}, u32[]{:S(2)}) collective-permute-start(f32[2,2,1,1,32,2048]{5,4,3,2,1,0:T(8,128)S(1)} %constant_dynamic-slice_fusion.17), channel_id=1, source_target_pairs={{0,2},{1,3},{2,0},{3,1},{4,6},{5,7},{6,4},{7,5},{8,10},{9,11},{10,... | collective-permute-start | bytes 3145736 | tf_op jit(solution)/shard_map/ppermute | solution.py:98
  988.5 32.7 %collective-permute-start.67 = (bf16[2,2,2,1,128,512]{5,4,3,2,1,0:T(8,128)(2,1)S(1)}, bf16[2,2,2,1,128,512]{5,4,3,2,1,0:T(8,128)(2,1)S(1)}, u32[]{:S(2)}, u32[]{:S(2)}) collective-permute-start(bf16[2,2,2,1,128,512]{5,4,3,2,1,0:T(8,128)(2,1)S(1)} %constant_dynamic-slice_fusion.18), channel_id=1, source_target_pairs={{0,1},{1,0},{2,3},{3,2},{4,5},{5,4},{6,7},{7,6},{8,9},{9,8},{10,11... | collective-permute-start | bytes 3145736 | tf_op jit(solution)/shard_map/ppermute | solution.py:98
  990.1 31.1 %collective-permute-start.66 = (bf16[2,2,2,1,32,2048]{5,4,3,2,1,0:T(8,128)(2,1)S(1)}, bf16[2,2,2,1,32,2048]{5,4,3,2,1,0:T(8,128)(2,1)S(1)}, u32[]{:S(2)}, u32[]{:S(2)}) collective-permute-start(bf16[2,2,2,1,32,2048]{5,4,3,2,1,0:T(8,128)(2,1)S(1)} %constant_dynamic-slice_fusion.19), channel_id=1, source_target_pairs={{0,1},{1,0},{2,3},{3,2},{4,5},{5,4},{6,7},{7,6},{8,9},{9,8},{10,11... | collective-permute-start | bytes 3145736 | tf_op jit(solution)/shard_map/ppermute | solution.py:98
  1023.1 47.0 %collective-permute-start.77 = (f32[1,1,2,1,128,512]{5,4,3,2,1,0:T(8,128)S(1)}, f32[1,1,2,1,128,512]{5,4,3,2,1,0:T(8,128)S(1)}, u32[]{:S(2)}, u32[]{:S(2)}) collective-permute-start(f32[1,1,2,1,128,512]{5,4,3,2,1,0:T(8,128)S(1)} %constant_dynamic-slice_fusion.8), channel_id=1, source_target_pairs={{0,4},{1,5},{2,6},{3,7},{4,0},{5,1},{6,2},{7,3},{8,12},{9,13},{10,... | collective-permute-start | bytes 1572872 | tf_op jit(solution)/shard_map/ppermute | solution.py:98
  1025.0 45.1 %collective-permute-start.75 = (f32[1,2,2,1,128,512]{5,4,3,2,1,0:T(8,128)S(1)}, f32[1,2,2,1,128,512]{5,4,3,2,1,0:T(8,128)S(1)}, u32[]{:S(2)}, u32[]{:S(2)}) collective-permute-start(f32[1,2,2,1,128,512]{5,4,3,2,1,0:T(8,128)S(1)} %constant_dynamic-slice_fusion.10), channel_id=1, source_target_pairs={{0,8},{1,9},{2,10},{3,11},{4,12},{5,13},{6,14},{7,15},{8,0},{9,1},... | collective-permute-start | bytes 3145736 | tf_op jit(solution)/shard_map/ppermute | solution.py:98
  1026.0 44.1 %collective-permute-start.74 = (f32[2,2,1,1,32,2048]{5,4,3,2,1,0:T(8,128)S(1)}, f32[2,2,1,1,32,2048]{5,4,3,2,1,0:T(8,128)S(1)}, u32[]{:S(2)}, u32[]{:S(2)}) collective-permute-start(f32[2,2,1,1,32,2048]{5,4,3,2,1,0:T(8,128)S(1)} %constant_dynamic-slice_fusion.11), channel_id=1, source_target_pairs={{0,2},{1,3},{2,0},{3,1},{4,6},{5,7},{6,4},{7,5},{8,10},{9,11},{10,... | collective-permute-start | bytes 3145736 | tf_op jit(solution)/shard_map/ppermute | solution.py:98
  1026.8 43.3 %collective-permute-start.76 = (f32[2,1,1,1,32,2048]{5,4,3,2,1,0:T(8,128)S(1)}, f32[2,1,1,1,32,2048]{5,4,3,2,1,0:T(8,128)S(1)}, u32[]{:S(2)}, u32[]{:S(2)}) collective-permute-start(f32[2,1,1,1,32,2048]{5,4,3,2,1,0:T(8,128)S(1)} %constant_dynamic-slice_fusion.9), channel_id=1, source_target_pairs={{0,4},{1,5},{2,6},{3,7},{4,0},{5,1},{6,2},{7,3},{8,12},{9,13},{10,... | collective-permute-start | bytes 1572872 | tf_op jit(solution)/shard_map/ppermute | solution.py:98
  1035.9 34.2 %collective-permute-start.78 = (f32[1,1,1,1,32,2048]{5,4,3,2,1,0:T(8,128)S(1)}, f32[1,1,1,1,32,2048]{5,4,3,2,1,0:T(8,128)S(1)}, u32[]{:S(2)}, u32[]{:S(2)}) collective-permute-start(f32[1,1,1,1,32,2048]{5,4,3,2,1,0:T(8,128)S(1)} %constant_dynamic-slice_fusion.7), channel_id=1, source_target_pairs={{0,8},{1,9},{2,10},{3,11},{4,12},{5,13},{6,14},{7,15},{8,0},{9,1},... | collective-permute-start | bytes 786440 | tf_op jit(solution)/shard_map/ppermute | solution.py:98
  1071.6 26.1 %collective-permute-start.81 = (f32[1,1,2,1,128,512]{5,4,3,2,1,0:T(8,128)S(1)}, f32[1,1,2,1,128,512]{5,4,3,2,1,0:T(8,128)S(1)}, u32[]{:S(2)}, u32[]{:S(2)}) collective-permute-start(f32[1,1,2,1,128,512]{5,4,3,2,1,0:T(8,128)S(1)} %constant_dynamic-slice_fusion.4), channel_id=1, source_target_pairs={{0,4},{1,5},{2,6},{3,7},{4,0},{5,1},{6,2},{7,3},{8,12},{9,13},{10,... | collective-permute-start | bytes 1572872 | tf_op jit(solution)/shard_map/ppermute | solution.py:98
  1072.4 42.8 %collective-permute-start.80 = (f32[2,1,1,1,32,2048]{5,4,3,2,1,0:T(8,128)S(1)}, f32[2,1,1,1,32,2048]{5,4,3,2,1,0:T(8,128)S(1)}, u32[]{:S(2)}, u32[]{:S(2)}) collective-permute-start(f32[2,1,1,1,32,2048]{5,4,3,2,1,0:T(8,128)S(1)} %constant_dynamic-slice_fusion.5), channel_id=1, source_target_pairs={{0,4},{1,5},{2,6},{3,7},{4,0},{5,1},{6,2},{7,3},{8,12},{9,13},{10,... | collective-permute-start | bytes 1572872 | tf_op jit(solution)/shard_map/ppermute | solution.py:98
  1133.0 182.9 %all-gather.9.cloned.1.call-start = ((), (), s32[]{:S(2)}) async-start(), calls=%async_computation.2 | async-start | bytes 22282240 | tf_op jit(solution)/shard_map/all_gather | solution.py:123
  (316 other events, 2868.3 us)
Sparse Core Ops, SparseCore 0:
  916.4 96.7 all-gather.6
  1015.5 98.1 all-gather.4
  1133.1 89.5 all-gather.10
  1225.4 90.4 all-gather.8
